TPU v7x, 32 devices: a whole 2x2x4 slice. The times are simulated.
32 devices in a mesh: zero: 8 (over y, x, core), width: 4 (over z).
Axes of the slice: x: 2, y: 2, z: 4, core: 2. Of those that a mesh axis runs over, the one named last changes fastest.
Arguments:
- train_query: bfloat16 [4608, 4096], P('zero', 'width'), may hold values from -0.09375 to 0.09375
- low_query: bfloat16 [4608, 64], P('zero'), may hold values from -0.09375 to 0.09375
- high_query: bfloat16 [64, 4096], P(None, 'width'), may hold values from -0.75 to 0.75
- train_key: bfloat16 [4608, 2048], P('zero', 'width'), may hold values from -0.09375 to 0.09375
- low_key: bfloat16 [4608, 64], P('zero'), may hold values from -0.09375 to 0.09375
- high_key: bfloat16 [64, 2048], P(None, 'width'), may hold values from -0.75 to 0.75
- train_value: bfloat16 [4608, 2048], P('zero', 'width'), may hold values from -0.09375 to 0.09375
- low_value: bfloat16 [4608, 64], P('zero'), may hold values from -0.09375 to 0.09375
- high_value: bfloat16 [64, 2048], P(None, 'width'), may hold values from -0.75 to 0.75
- train_mixed: bfloat16 [4096, 4608], P('width', 'zero'), may hold values from -0.09375 to 0.09375
- low_mixed: bfloat16 [4096, 64], P('width'), may hold values from -0.09375 to 0.09375
- high_mixed: bfloat16 [64, 4608], P(None, 'zero'), may hold values from -0.75 to 0.75
- norm_train: float32 [4608], P(('zero', 'width')), may hold values from 0.25 to 1.75
- norm_step: float32 [4608], P(('zero', 'width')), may hold values from -0.3 to 0.3
Outputs:
- final_query: bfloat16 [4608, 4096], P(None, 'width')
- final_key: bfloat16 [4608, 2048], P(None, 'width')
- final_value: bfloat16 [4608, 2048], P(None, 'width')
- final_mixed: bfloat16 [4096, 4608], P('width')
- serve_norm: bfloat16 [4608], replicated
All inputs are finite; a program needn't handle non-finite values.
Results may differ from a plain program's by a relative error of at most 0.001.
Values may be sent and summed in bfloat16 or wider, within the bound.
A program may use at most 192 MiB of HBM per device.

v0:
```python
import jax
import jax.numpy as jnp
from jax import lax
from jax.sharding import PartitionSpec as P

mix_rate = 0.5


def on_device(
    train_query,
    low_query,
    high_query,
    train_key,
    low_key,
    high_key,
    train_value,
    low_value,
    high_value,
    train_mixed,
    low_mixed,
    high_mixed,
    norm_train,
    norm_step,
):
    (
        moved_query,
        moved_key,
        moved_value,
        moved_mixed,
        factor_query,
        factor_key,
        factor_value,
        factor_mixed,
    ) = (
        lax.all_gather(train_query, "zero", axis=0, tiled=True),
        lax.all_gather(train_key, "zero", axis=0, tiled=True),
        lax.all_gather(train_value, "zero", axis=0, tiled=True),
        lax.all_gather(train_mixed, "zero", axis=1, tiled=True),
        lax.all_gather(low_query, "zero", axis=0, tiled=True),
        lax.all_gather(low_key, "zero", axis=0, tiled=True),
        lax.all_gather(low_value, "zero", axis=0, tiled=True),
        lax.all_gather(high_mixed, "zero", axis=1, tiled=True),
    )
    result_query = moved_query.astype(jnp.float32) + mix_rate * jnp.dot(
        factor_query, high_query, preferred_element_type=jnp.float32
    )
    final_query = result_query.astype(jnp.bfloat16)
    result_key = moved_key.astype(jnp.float32) + mix_rate * jnp.dot(
        factor_key, high_key, preferred_element_type=jnp.float32
    )
    final_key = result_key.astype(jnp.bfloat16)
    result_value = moved_value.astype(jnp.float32) + mix_rate * jnp.dot(
        factor_value, high_value, preferred_element_type=jnp.float32
    )
    final_value = result_value.astype(jnp.bfloat16)
    result_mixed = moved_mixed.astype(jnp.float32) + mix_rate * jnp.dot(
        low_mixed, factor_mixed, preferred_element_type=jnp.float32
    )
    final_mixed = result_mixed.astype(jnp.bfloat16)
    serve_norm = lax.all_gather(
        (norm_train + norm_step).astype(jnp.bfloat16), ("zero", "width"), axis=0, tiled=True
    )
    return (final_query, final_key, final_value, final_mixed, serve_norm)


def solution(mesh):
    return jax.shard_map(
        on_device,
        mesh=mesh,
        in_specs=(
            P("zero", "width"),
            P("zero", None),
            P(None, "width"),
            P("zero", "width"),
            P("zero", None),
            P(None, "width"),
            P("zero", "width"),
            P("zero", None),
            P(None, "width"),
            P("width", "zero"),
            P("width", None),
            P(None, "zero"),
            P(("zero", "width")),
            P(("zero", "width")),
        ),
        out_specs=(P(None, "width"), P(None, "width"), P(None, "width"), P("width", None), P()),
        check_vma=False,
    )
```

profile of v0, /device:TPU:0, one launch (start us, length us, event | category | flops | bytes accessed | tf_op | source)
XLA Modules:
  0.0 232.1 jit_solution(15176679643474011088)
XLA Ops:
  7.2 0.0 copy-start
  7.2 0.0 copy-start.2
  7.2 0.0 copy-start.3
  7.2 0.0 copy-start.6
  7.2 0.0 copy-start.7
  7.2 0.0 copy-start.4
  7.2 0.0 all-gather.13.cloned.1.call-start
  7.3 0.7 all-gather.13.cloned.1.call-update
  8.0 0.0 all-gather.11.cloned.1.call-start
  8.0 0.7 all-gather.11.cloned.1.call-update
  8.7 0.0 all-gather.15.cloned.1.call-start
  8.8 0.7 all-gather.15.cloned.1.call-update
  9.5 0.0 all-gather.9.cloned.1.call-start
  9.5 0.5 all-gather.9.cloned.1.call-update
  10.0 12.0 %all-gather.3 = bf16[8,576,64]{1,2,0:T(8,128)(2,1)S(1)} all-gather(bf16[1,576,64]{1,2,0:T(8,128)(2,1)} %bitcast.22), channel_id=1, replica_groups=mesh['zero'=8,'width'=4] {'zero'}, dimensions={0}, use_global_device_ids=true | all-gather | bytes 663552 | tf_op jit(solution)/shard_map/all_gather | solution.py:42
  22.0 0.4 copy.29
  22.4 0.4 reshape.19
  22.8 10.9 %all-gather = bf16[8,576,64]{1,2,0:T(8,128)(2,1)S(1)} all-gather(bf16[1,576,64]{1,2,0:T(8,128)(2,1)} %bitcast.23), channel_id=1, replica_groups=mesh['zero'=8,'width'=4] {'zero'}, dimensions={0}, use_global_device_ids=true | all-gather | bytes 663552 | tf_op jit(solution)/shard_map/all_gather | solution.py:39
  33.7 0.0 copy-start.5
  33.7 0.4 copy.25
  34.1 0.4 reshape.13
  34.5 0.0 copy-done.2
  34.5 13.3 %all-gather.2 = bf16[8,576,64]{1,2,0:T(8,128)(2,1)S(1)} all-gather(bf16[1,576,64]{1,2,0:T(8,128)(2,1)S(1)} %bitcast.24), channel_id=1, replica_groups=mesh['zero'=8,'width'=4] {'zero'}, dimensions={0}, use_global_device_ids=true | all-gather | bytes 663552 | tf_op jit(solution)/shard_map/all_gather | solution.py:41
  47.8 0.4 copy.27
  48.2 0.4 reshape.17
  48.6 0.0 copy-done.3
  48.6 10.3 %all-gather.1 = bf16[8,576,64]{1,2,0:T(8,128)(2,1)S(1)} all-gather(bf16[1,576,64]{1,2,0:T(8,128)(2,1)S(1)} %bitcast.25), channel_id=1, replica_groups=mesh['zero'=8,'width'=4] {'zero'}, dimensions={0}, use_global_device_ids=true | all-gather | bytes 663552 | tf_op jit(solution)/shard_map/all_gather | solution.py:40
  58.9 0.4 copy.26
  59.3 0.4 reshape.15
  59.7 0.0 copy-done.6
  59.7 0.0 copy-done.7
  59.8 0.2 dynamic-update-slice
  60.0 40.2 %all-reduce = bf16[4608]{0:T(1024)(128)(2,1)} all-reduce(bf16[4608]{0:T(1024)(128)(2,1)S(1)} %dynamic-update-slice), channel_id=1, replica_groups=mesh['zero'=8,'width'=4] {'zero','width'}, use_global_device_ids=true, to_apply=%add | all-reduce | flops 4608 | bytes 18432
  100.2 0.0 all-gather.13.cloned.1.call-done
  100.2 0.0 copy-done.4
  100.2 5.9 %add_convert_fusion.2 = bf16[4608,512]{1,0:T(8,128)(2,1)} fusion(bf16[4608,512]{1,0:T(8,128)(2,1)} %all-gather.13.cloned.1.call-done, bf16[4608,64]{0,1:T(8,128)(2,1)S(1)} %reshape.17, bf16[64,512]{1,0:T(8,128)(2,1)S(1)} %copy-done.4), kind=kOutput, calls=%fused_computation.2 | convolution fusion | flops 311427072 | bytes 10092544 | tf_op jit(solution)/shard_map/dot_general | solution.py:52
  106.2 0.0 all-gather.11.cloned.1.call-done
  106.2 0.0 copy-done.5
  106.2 6.4 %add_convert_fusion.3 = bf16[4608,512]{1,0:T(8,128)(2,1)} fusion(bf16[4608,512]{1,0:T(8,128)(2,1)} %all-gather.11.cloned.1.call-done, bf16[4608,64]{0,1:T(8,128)(2,1)S(1)} %reshape.15, bf16[64,512]{1,0:T(8,128)(2,1)S(1)} %copy-done.5), kind=kOutput, calls=%fused_computation.3 | convolution fusion | flops 311427072 | bytes 10092544 | tf_op jit(solution)/shard_map/dot_general | solution.py:48
  112.6 45.0 %all-gather.15.cloned.1.call-done = bf16[1024,4608]{0,1:T(8,128)(2,1)} async-done(((bf16[1024,576]{0,1:T(8,128)(2,1)}), bf16[1024,4608]{0,1:T(8,128)(2,1)}) %all-gather.15.cloned.1.call-update) | async-done | bytes 9437200 | tf_op jit(solution)/shard_map/all_gather | solution.py:38
  157.6 12.7 %copy.28 = bf16[1024,4608]{1,0:T(8,128)(2,1)} copy(bf16[1024,4608]{0,1:T(8,128)(2,1)} %all-gather.15.cloned.1.call-done) | data formatting | bytes 18874368 | tf_op jit(solution)/shard_map/all_gather | solution.py:38
  170.3 0.0 copy-done
  170.3 0.0 copy-start.1
  170.3 7.5 %add_convert_fusion = bf16[1024,4608]{1,0:T(8,128)(2,1)} fusion(bf16[1024,4608]{1,0:T(8,128)(2,1)} %copy.28, bf16[1024,64]{0,1:T(8,128)(2,1)S(1)} %copy-done, bf16[4608,64]{0,1:T(8,128)(2,1)S(1)} %reshape.19), kind=kOutput, calls=%fused_computation | convolution fusion | flops 622854144 | bytes 19595264 | tf_op jit(solution)/shard_map/dot_general | solution.py:56
  177.8 40.2 %all-gather.9.cloned.1.call-done = bf16[4608,1024]{1,0:T(8,128)(2,1)} async-done(((bf16[576,1024]{1,0:T(8,128)(2,1)}), bf16[4608,1024]{1,0:T(8,128)(2,1)}) %all-gather.9.cloned.1.call-update) | async-done | bytes 9437200 | tf_op jit(solution)/shard_map/all_gather | solution.py:35
  218.1 0.0 copy-done.1
  218.1 7.5 %add_convert_fusion.1 = bf16[4608,1024]{1,0:T(8,128)(2,1)} fusion(bf16[4608,1024]{1,0:T(8,128)(2,1)} %all-gather.9.cloned.1.call-done, bf16[4608,64]{0,1:T(8,128)(2,1)S(1)} %reshape.13, bf16[64,1024]{1,0:T(8,128)(2,1)S(1)} %copy-done.1), kind=kOutput, calls=%fused_computation.1 | convolution fusion | flops 622854144 | bytes 19595264 | tf_op jit(solution)/shard_map/dot_general | solution.py:44
  (2 shorter events, 0.0 us)
Async XLA Ops:
  7.2 163.1 %copy-start = (bf16[1024,64]{0,1:T(8,128)(2,1)S(1)}, bf16[1024,64]{0,1:T(8,128)(2,1)}, u32[]{:S(2)}) copy-start(bf16[1024,64]{0,1:T(8,128)(2,1)} %param.24) | copy-start | bytes 393220
  7.2 27.4 %copy-start.2 = (bf16[576,64]{0,1:T(8,128)(2,1)S(1)}, bf16[576,64]{0,1:T(8,128)(2,1)}, u32[]{:S(2)}) copy-start(bf16[576,64]{0,1:T(8,128)(2,1)} %param.21) | copy-start | bytes 221188
  7.2 41.4 %copy-start.3 = (bf16[576,64]{0,1:T(8,128)(2,1)S(1)}, bf16[576,64]{0,1:T(8,128)(2,1)}, u32[]{:S(2)}) copy-start(bf16[576,64]{0,1:T(8,128)(2,1)} %param.18) | copy-start | bytes 221188
  7.2 52.5 %copy-start.6 = (f32[144]{0:T(256)S(1)}, f32[144]{0:T(256)}, u32[]{:S(2)}) copy-start(f32[144]{0:T(256)} %param.26) | copy-start | bytes 1732
  7.2 52.5 %copy-start.7 = (f32[144]{0:T(256)S(1)}, f32[144]{0:T(256)}, u32[]{:S(2)}) copy-start(f32[144]{0:T(256)} %param.27) | copy-start | bytes 1732
  7.2 93.0 %copy-start.4 = (bf16[64,512]{1,0:T(8,128)(2,1)S(1)}, bf16[64,512]{1,0:T(8,128)(2,1)}, u32[]{:S(2)}) copy-start(bf16[64,512]{1,0:T(8,128)(2,1)} %param.22) | copy-start | bytes 196612
  7.2 93.0 %all-gather.13.cloned.1.call-start = ((), (), s32[]{:S(2)}) async-start(), calls=%async_computation.2 | async-start | bytes 5308416 | tf_op jit(solution)/shard_map/all_gather | solution.py:37
  8.0 98.2 %all-gather.11.cloned.1.call-start = ((), (), s32[]{:S(2)}) async-start(), calls=%async_computation.1 | async-start | bytes 5308416 | tf_op jit(solution)/shard_map/all_gather | solution.py:36
  8.7 148.9 %all-gather.15.cloned.1.call-start = ((), (), s32[]{:S(2)}) async-start(), calls=%async_computation.3 | async-start | bytes 10616832 | tf_op jit(solution)/shard_map/all_gather | solution.py:38
  9.5 208.6 %all-gather.9.cloned.1.call-start = ((), (), s32[]{:S(2)}) async-start(), calls=%async_computation | async-start | bytes 10616832 | tf_op jit(solution)/shard_map/all_gather | solution.py:35
  33.7 72.4 %copy-start.5 = (bf16[64,512]{1,0:T(8,128)(2,1)S(1)}, bf16[64,512]{1,0:T(8,128)(2,1)}, u32[]{:S(2)}) copy-start(bf16[64,512]{1,0:T(8,128)(2,1)} %param.19) | copy-start | bytes 196612
  170.3 47.8 %copy-start.1 = (bf16[64,1024]{1,0:T(8,128)(2,1)S(1)}, bf16[64,1024]{1,0:T(8,128)(2,1)}, u32[]{:S(2)}) copy-start(bf16[64,1024]{1,0:T(8,128)(2,1)} %param.16) | copy-start | bytes 393220
Sparse Core Ops, SparseCore 0:
  9.9 45.4 all-gather.12
  57.3 39.6 all-gather.10
  98.9 58.6 all-gather.14
  159.3 58.6 all-gather.8
where the time goes:
time: 233 us; the launch traced here: 232 us
  waiting for transfers between devices  87.8 us (38%)
  blocking collectives  86.6 us (37%)
  matrix products  27.4 us (12%)
  local copies, waits for them, and re-layouts  16.2 us (7%)
  between operations  13.9 us (6%)
    all_gather x1, waiting for transfers between devices, on_device(): lax.all_gather(train_mixed, 'zero', axis=1, tiled=True)  45 us
    all_gather x1, waiting for transfers between devices, on_device(): lax.all_gather(train_query, 'zero', axis=0, tiled=True)  40.2 us
    unnamed x1, blocking collectives  40.2 us
    all_gather x1, blocking collectives, on_device(): lax.all_gather(low_value, 'zero', axis=0, tiled=True)  13.3 us
    all_gather x1, local copies, waits for them, and re-layouts, on_device(): lax.all_gather(train_mixed, 'zero', axis=1, tiled=True)  12.7 us
    all_gather x1, blocking collectives, on_device(): lax.all_gather(high_mixed, 'zero', axis=1, tiled=True)  12 us
    all_gather x1, blocking collectives, on_device(): lax.all_gather(low_query, 'zero', axis=0, tiled=True)  10.9 us
    all_gather x1, blocking collectives, on_device(): lax.all_gather(low_key, 'zero', axis=0, tiled=True)  10.3 us
  transfers between devices with their start and end apart: 4, of which 2 were waited for; matrix products, arithmetic and copies ran while one was open for 16% of the time, Pallas kernels for 0%

commit v1 on v0

--- a/solution.py
+++ b/solution.py
@@ -4,6 +4,12 @@
 from jax.sharding import PartitionSpec as P
 
 mix_rate = 0.5
+
+
+def gather_blocks(block, axis, along):
+    parts = lax.all_gather(block, axis, axis=0, tiled=False)
+    whole = jnp.concatenate(parts, axis=along)
+    return whole
 
 
 def on_device(
@@ -39,7 +45,7 @@
         lax.all_gather(low_query, "zero", axis=0, tiled=True),
         lax.all_gather(low_key, "zero", axis=0, tiled=True),
         lax.all_gather(low_value, "zero", axis=0, tiled=True),
-        lax.all_gather(high_mixed, "zero", axis=1, tiled=True),
+        gather_blocks(high_mixed, "zero", 1),
     )
     result_query = moved_query.astype(jnp.float32) + mix_rate * jnp.dot(
         factor_query, high_query, preferred_element_type=jnp.float32

time: 233 us -> 233 us (level)
  no operation moved by 1% of the time
where the time goes in v1:
time: 233 us; the launch traced here: 232 us
  waiting for transfers between devices  87.8 us (38%)
  blocking collectives  86.6 us (37%)
  matrix products  27.4 us (12%)
  local copies, waits for them, and re-layouts  16.2 us (7%)
  between operations  13.9 us (6%)
    all_gather x1, waiting for transfers between devices, on_device(): lax.all_gather(train_mixed, 'zero', axis=1, tiled=True)  45 us
    all_gather x1, waiting for transfers between devices, on_device(): lax.all_gather(train_query, 'zero', axis=0, tiled=True)  40.2 us
    unnamed x1, blocking collectives  40.2 us
    all_gather x1, blocking collectives, on_device(): lax.all_gather(low_value, 'zero', axis=0, tiled=True)  13.3 us
    all_gather x1, local copies, waits for them, and re-layouts, on_device(): lax.all_gather(train_mixed, 'zero', axis=1, tiled=True)  12.7 us
    all_gather x1, blocking collectives, gather_blocks(): parts = lax.all_gather(block, axis, axis=0, tiled=False)  12 us
    all_gather x1, blocking collectives, on_device(): lax.all_gather(low_query, 'zero', axis=0, tiled=True)  10.9 us
    all_gather x1, blocking collectives, on_device(): lax.all_gather(low_key, 'zero', axis=0, tiled=True)  10.3 us
  transfers between devices with their start and end apart: 4, of which 2 were waited for; matrix products, arithmetic and copies ran while one was open for 16% of the time, Pallas kernels for 0%

profile of v1, /device:TPU:0, one launch (start us, length us, event | category | flops | bytes accessed | tf_op | source)
XLA Modules:
  0.0 232.1 jit_solution(972469299460035419)
XLA Ops:
  7.2 0.0 copy-start
  7.2 0.0 copy-start.2
  7.2 0.0 copy-start.3
  7.2 0.0 copy-start.6
  7.2 0.0 copy-start.7
  7.2 0.0 copy-start.4
  7.2 0.0 all-gather.13.cloned.1.call-start
  7.3 0.7 all-gather.13.cloned.1.call-update
  8.0 0.0 all-gather.11.cloned.1.call-start
  8.0 0.7 all-gather.11.cloned.1.call-update
  8.7 0.0 all-gather.15.cloned.1.call-start
  8.8 0.7 all-gather.15.cloned.1.call-update
  9.5 0.0 all-gather.9.cloned.1.call-start
  9.5 0.5 all-gather.9.cloned.1.call-update
  10.0 12.0 %all-gather = bf16[512,576]{1,0:T(8,128)(2,1)S(1)} all-gather(bf16[64,576]{1,0:T(8,128)(2,1)} %param.25), channel_id=2, replica_groups=mesh['zero'=8,'width'=4] {'zero'}, dimensions={0}, use_global_device_ids=true | all-gather | bytes 663552 | tf_op jit(solution)/shard_map/all_gather | solution.py:10
  22.0 0.4 copy.31
  22.4 0.4 reshape.17
  22.8 10.9 %all-gather.1 = bf16[8,576,64]{1,2,0:T(8,128)(2,1)S(1)} all-gather(bf16[1,576,64]{1,2,0:T(8,128)(2,1)} %bitcast.23), channel_id=1, replica_groups=mesh['zero'=8,'width'=4] {'zero'}, dimensions={0}, use_global_device_ids=true | all-gather | bytes 663552 | tf_op jit(solution)/shard_map/all_gather | solution.py:45
  33.7 0.0 copy-start.5
  33.7 0.4 copy.25
  34.1 0.4 reshape.22
  34.5 0.0 copy-done.2
  34.5 13.3 %all-gather.3 = bf16[8,576,64]{1,2,0:T(8,128)(2,1)S(1)} all-gather(bf16[1,576,64]{1,2,0:T(8,128)(2,1)S(1)} %bitcast.24), channel_id=1, replica_groups=mesh['zero'=8,'width'=4] {'zero'}, dimensions={0}, use_global_device_ids=true | all-gather | bytes 663552 | tf_op jit(solution)/shard_map/all_gather | solution.py:47
  47.8 0.4 copy.27
  48.2 0.4 reshape.26
  48.6 0.0 copy-done.3
  48.6 10.3 %all-gather.2 = bf16[8,576,64]{1,2,0:T(8,128)(2,1)S(1)} all-gather(bf16[1,576,64]{1,2,0:T(8,128)(2,1)S(1)} %bitcast.25), channel_id=1, replica_groups=mesh['zero'=8,'width'=4] {'zero'}, dimensions={0}, use_global_device_ids=true | all-gather | bytes 663552 | tf_op jit(solution)/shard_map/all_gather | solution.py:46
  58.9 0.4 copy.26
  59.3 0.4 reshape.24
  59.7 0.0 copy-done.6
  59.7 0.0 copy-done.7
  59.8 0.2 dynamic-update-slice
  60.0 40.2 %all-reduce = bf16[4608]{0:T(1024)(128)(2,1)} all-reduce(bf16[4608]{0:T(1024)(128)(2,1)S(1)} %dynamic-update-slice), channel_id=1, replica_groups=mesh['zero'=8,'width'=4] {'zero','width'}, use_global_device_ids=true, to_apply=%add | all-reduce | flops 4608 | bytes 18432
  100.2 0.0 all-gather.13.cloned.1.call-done
  100.2 0.0 copy-done.4
  100.2 5.9 %add_convert_fusion.2 = bf16[4608,512]{1,0:T(8,128)(2,1)} fusion(bf16[4608,512]{1,0:T(8,128)(2,1)} %all-gather.13.cloned.1.call-done, bf16[4608,64]{0,1:T(8,128)(2,1)S(1)} %reshape.26, bf16[64,512]{1,0:T(8,128)(2,1)S(1)} %copy-done.4), kind=kOutput, calls=%fused_computation.2 | convolution fusion | flops 311427072 | bytes 10092544 | tf_op jit(solution)/shard_map/dot_general | solution.py:58
  106.2 0.0 all-gather.11.cloned.1.call-done
  106.2 0.0 copy-done.5
  106.2 6.4 %add_convert_fusion.3 = bf16[4608,512]{1,0:T(8,128)(2,1)} fusion(bf16[4608,512]{1,0:T(8,128)(2,1)} %all-gather.11.cloned.1.call-done, bf16[4608,64]{0,1:T(8,128)(2,1)S(1)} %reshape.24, bf16[64,512]{1,0:T(8,128)(2,1)S(1)} %copy-done.5), kind=kOutput, calls=%fused_computation.3 | convolution fusion | flops 311427072 | bytes 10092544 | tf_op jit(solution)/shard_map/dot_general | solution.py:54
  112.6 45.0 %all-gather.15.cloned.1.call-done = bf16[1024,4608]{0,1:T(8,128)(2,1)} async-done(((bf16[1024,576]{0,1:T(8,128)(2,1)}), bf16[1024,4608]{0,1:T(8,128)(2,1)}) %all-gather.15.cloned.1.call-update) | async-done | bytes 9437200 | tf_op jit(solution)/shard_map/all_gather | solution.py:44
  157.6 12.7 %copy.28 = bf16[1024,4608]{1,0:T(8,128)(2,1)} copy(bf16[1024,4608]{0,1:T(8,128)(2,1)} %all-gather.15.cloned.1.call-done) | data formatting | bytes 18874368 | tf_op jit(solution)/shard_map/all_gather | solution.py:44
  170.3 0.0 copy-done
  170.3 0.0 copy-start.1
  170.3 7.5 %add_convert_fusion = bf16[1024,4608]{1,0:T(8,128)(2,1)} fusion(bf16[1024,4608]{1,0:T(8,128)(2,1)} %copy.28, bf16[1024,64]{0,1:T(8,128)(2,1)S(1)} %copy-done, bf16[64,4608]{1,0:T(8,128)(2,1)S(1)} %reshape.17), kind=kOutput, calls=%fused_computation | convolution fusion | flops 622854144 | bytes 19595264 | tf_op jit(solution)/shard_map/dot_general | solution.py:62
  177.8 40.2 %all-gather.9.cloned.1.call-done = bf16[4608,1024]{1,0:T(8,128)(2,1)} async-done(((bf16[576,1024]{1,0:T(8,128)(2,1)}), bf16[4608,1024]{1,0:T(8,128)(2,1)}) %all-gather.9.cloned.1.call-update) | async-done | bytes 9437200 | tf_op jit(solution)/shard_map/all_gather | solution.py:41
  218.1 0.0 copy-done.1
  218.1 7.5 %add_convert_fusion.1 = bf16[4608,1024]{1,0:T(8,128)(2,1)} fusion(bf16[4608,1024]{1,0:T(8,128)(2,1)} %all-gather.9.cloned.1.call-done, bf16[4608,64]{0,1:T(8,128)(2,1)S(1)} %reshape.22, bf16[64,1024]{1,0:T(8,128)(2,1)S(1)} %copy-done.1), kind=kOutput, calls=%fused_computation.1 | convolution fusion | flops 622854144 | bytes 19595264 | tf_op jit(solution)/shard_map/dot_general | solution.py:50
  (2 shorter events, 0.0 us)
Async XLA Ops:
  7.2 163.1 %copy-start = (bf16[1024,64]{0,1:T(8,128)(2,1)S(1)}, bf16[1024,64]{0,1:T(8,128)(2,1)}, u32[]{:S(2)}) copy-start(bf16[1024,64]{0,1:T(8,128)(2,1)} %param.24) | copy-start | bytes 393220
  7.2 27.4 %copy-start.2 = (bf16[576,64]{0,1:T(8,128)(2,1)S(1)}, bf16[576,64]{0,1:T(8,128)(2,1)}, u32[]{:S(2)}) copy-start(bf16[576,64]{0,1:T(8,128)(2,1)} %param.21) | copy-start | bytes 221188
  7.2 41.4 %copy-start.3 = (bf16[576,64]{0,1:T(8,128)(2,1)S(1)}, bf16[576,64]{0,1:T(8,128)(2,1)}, u32[]{:S(2)}) copy-start(bf16[576,64]{0,1:T(8,128)(2,1)} %param.18) | copy-start | bytes 221188
  7.2 52.5 %copy-start.6 = (f32[144]{0:T(256)S(1)}, f32[144]{0:T(256)}, u32[]{:S(2)}) copy-start(f32[144]{0:T(256)} %param.26) | copy-start | bytes 1732
  7.2 52.5 %copy-start.7 = (f32[144]{0:T(256)S(1)}, f32[144]{0:T(256)}, u32[]{:S(2)}) copy-start(f32[144]{0:T(256)} %param.27) | copy-start | bytes 1732
  7.2 93.0 %copy-start.4 = (bf16[64,512]{1,0:T(8,128)(2,1)S(1)}, bf16[64,512]{1,0:T(8,128)(2,1)}, u32[]{:S(2)}) copy-start(bf16[64,512]{1,0:T(8,128)(2,1)} %param.22) | copy-start | bytes 196612
  7.2 93.0 %all-gather.13.cloned.1.call-start = ((), (), s32[]{:S(2)}) async-start(), calls=%async_computation.2 | async-start | bytes 5308416 | tf_op jit(solution)/shard_map/all_gather | solution.py:43
  8.0 98.2 %all-gather.11.cloned.1.call-start = ((), (), s32[]{:S(2)}) async-start(), calls=%async_computation.1 | async-start | bytes 5308416 | tf_op jit(solution)/shard_map/all_gather | solution.py:42
  8.7 148.9 %all-gather.15.cloned.1.call-start = ((), (), s32[]{:S(2)}) async-start(), calls=%async_computation.3 | async-start | bytes 10616832 | tf_op jit(solution)/shard_map/all_gather | solution.py:44
  9.5 208.6 %all-gather.9.cloned.1.call-start = ((), (), s32[]{:S(2)}) async-start(), calls=%async_computation | async-start | bytes 10616832 | tf_op jit(solution)/shard_map/all_gather | solution.py:41
  33.7 72.4 %copy-start.5 = (bf16[64,512]{1,0:T(8,128)(2,1)S(1)}, bf16[64,512]{1,0:T(8,128)(2,1)}, u32[]{:S(2)}) copy-start(bf16[64,512]{1,0:T(8,128)(2,1)} %param.19) | copy-start | bytes 196612
  170.3 47.8 %copy-start.1 = (bf16[64,1024]{1,0:T(8,128)(2,1)S(1)}, bf16[64,1024]{1,0:T(8,128)(2,1)}, u32[]{:S(2)}) copy-start(bf16[64,1024]{1,0:T(8,128)(2,1)} %param.16) | copy-start | bytes 393220
Sparse Core Ops, SparseCore 0:
  9.9 45.4 all-gather.12
  57.3 39.6 all-gather.10
  98.9 58.6 all-gather.14
  159.3 58.6 all-gather.8
